TPU v7x, 256 devices: a 4x2x16 block of a 4x16x16 slice. The times are simulated.
256 devices in a mesh: groups: 2 (over y), gx: 32 (over z, core), gy: 4 (over x).
Axes of the slice: x: 4, y: 2, z: 16, core: 2. Of those that a mesh axis runs over, the one named last changes fastest.
The devices are a block of a 4x16x16 slice.
Arguments:
- hidden_in: bfloat16 [1024, 18432], P(('groups', 'gx'), 'gy'), parts along dimension 0, may hold values from -6 to 6
- w_query: bfloat16 [18432, 12288], P('gy', 'gx'), may hold values from -0.046875 to 0.046875
- w_out: bfloat16 [12288, 18432], P('gx', 'gy'), may hold values from -0.4375 to 0.4375
- cache_keys: bfloat16 [1024, 1024, 256], P(('groups', 'gx', 'gy')), parts along dimension 0, may hold values from -250 to 250
- cache_values: bfloat16 [1024, 1024, 256], P(('groups', 'gx', 'gy')), parts along dimension 0, may hold values from -6 to 6
- lengths: int32 [1024], P(('groups', 'gx', 'gy')), parts along dimension 0, may hold values from 128 to 1024
Outputs:
- layer_out: bfloat16 [1024, 18432], P(('groups', 'gx'), 'gy'), parts along dimension 0
There are 2 independent parts, one for each index of `groups`. A program takes and returns all parts, laid end to end along the dimension named above; an argument that names none is the same for every part. Nothing has to cross between parts.
All inputs are finite; a program needn't handle non-finite values.
Results may differ from a plain program's by a relative error of at most 0.0097.
Values may be sent and summed in bfloat16 or wider, within the bound.
A program may use at most 64 MiB of HBM per device.

v0:
```python
import jax
import jax.numpy as jnp
from jax import lax
from jax.sharding import Mesh
from jax.sharding import PartitionSpec as P

GX = ("gx_0", "gx_1")
GROUPS_GX = ("groups", "gx_0", "gx_1")
GROUPS_GX_GY = ("groups", "gx_0", "gx_1", "gy")


def cut_along(x, dim, size):
    dims = x.shape
    tiles = x.reshape(*dims[:dim], size, dims[dim] // size, *dims[dim + 1 :])
    return jnp.moveaxis(tiles, dim, 0)


def summed_on_arrival(x, axis, dim):
    size = lax.axis_size(axis)
    tiles = lax.all_to_all(cut_along(x, dim, size), axis, 0, 0, tiled=True)
    return jnp.sum(tiles, axis=0)


def reduced_to_own(tiles, axes, sequence):
    dims = [lax.axis_size(a) for a in axes]
    tiles = tiles.reshape(*dims, *tiles.shape[1:])
    tiles = tiles.transpose(*sequence, *range(len(axes), tiles.ndim))
    tiles = tiles.reshape(-1, *tiles.shape[len(axes) :])
    for k in sequence:
        tiles = lax.psum_scatter(tiles, axes[k], scatter_dimension=0, tiled=True)
    return tiles[0]


def sum_by_axis(x, axes, sequence, dim):
    size = lax.axis_size(axes)
    return reduced_to_own(cut_along(x, dim, size), axes, sequence)


def body(hidden_in, w_query, w_out, cache_keys, cache_values, lengths):
    across = lax.axis_size(GX)
    within = lax.axis_size("gy")
    local_seqs = cache_keys.shape[0]
    slot_count = cache_keys.shape[1]
    head_dim = cache_keys.shape[2]
    partial_query = jnp.dot(
        lax.all_gather(hidden_in, GX, axis=0, tiled=True),
        w_query,
        preferred_element_type=jnp.float32,
    )
    slice_width = partial_query.shape[1]
    grouped = partial_query.reshape(across, within, local_seqs, slice_width)
    own_rows = summed_on_arrival(grouped, "gy", 1)
    query_rows = own_rows.reshape(across * local_seqs, slice_width).astype(jnp.bfloat16)
    query = lax.all_to_all(query_rows, GX, split_axis=0, concat_axis=1, tiled=True)
    head_count = query.shape[1] // head_dim
    query_heads = query.reshape(local_seqs, head_count, head_dim)
    scores = jnp.einsum("bhd,bld->bhl", query_heads, cache_keys, preferred_element_type=jnp.float32)
    scores = scores / jnp.sqrt(jnp.float32(head_dim))
    live_slots = jnp.arange(slot_count)[None, None, :] < lengths[:, None, None]
    scores = jnp.where(live_slots, scores, jnp.float32(-1e30))
    top_score = jnp.max(scores, axis=2, keepdims=True)
    expo = jnp.where(live_slots, jnp.exp(scores - top_score), jnp.float32(0.0))
    probs = (expo / jnp.sum(expo, axis=2, keepdims=True)).astype(jnp.bfloat16)
    mixed = jnp.einsum("bhl,bld->bhd", probs, cache_values, preferred_element_type=jnp.float32)
    attended = mixed.astype(jnp.bfloat16).reshape(local_seqs, head_count * head_dim)
    spread = lax.all_to_all(attended, GX, split_axis=1, concat_axis=0, tiled=True)
    stacked = spread.reshape(across, local_seqs, slice_width)
    gathered = lax.all_gather(stacked, "gy", axis=1, tiled=True)
    head_rows = gathered.reshape(across * within * local_seqs, slice_width)
    result = sum_by_axis(
        jnp.dot(head_rows, w_out, preferred_element_type=jnp.float32), GX, (1, 0), 0
    )
    return result.astype(jnp.bfloat16)


def solution(mesh):
    torus = Mesh(
        mesh.devices.reshape(mesh.shape["groups"], 16, 2, mesh.shape["gy"]),
        ("groups", "gx_0", "gx_1", "gy"),
    )
    placed = (
        P(GROUPS_GX, "gy"),
        P("gy", GX),
        P(GX, "gy"),
        P(GROUPS_GX_GY, None, None),
        P(GROUPS_GX_GY, None, None),
        P(GROUPS_GX_GY),
    )
    return jax.shard_map(
        body, mesh=torus, in_specs=placed, out_specs=P(GROUPS_GX, "gy"), check_vma=False
    )
```

profile of v0, /device:TPU:36, one launch (start us, length us, event | category | flops | bytes accessed | tf_op | source)
XLA Modules:
  0.0 308.4 jit_solution(460804432666121327)
XLA Ops:
  6.5 0.0 copy-start
  6.6 0.0 all-gather.2.cloned.1.call-start
  6.6 0.7 all-gather.2.cloned.1.call-update
  7.3 87.8 %all-gather.2.cloned.1.call-done = bf16[512,4608]{1,0:T(8,128)(2,1)} async-done(((bf16[16,4608]{1,0:T(8,128)(2,1)}), bf16[512,4608]{1,0:T(8,128)(2,1)}) %all-gather.2.cloned.1.call-update) | async-done | bytes 4718608 | tf_op jit(solution)/shard_map/all_gather | solution.py:46
  95.1 6.9 %fusion.10 = f32[512,384]{1,0:T(8,128)} fusion(bf16[512,4608]{1,0:T(8,128)(2,1)} %all-gather.2.cloned.1.call-done, bf16[4608,384]{1,0:T(8,128)(2,1)} %param.7), kind=kOutput, calls=%fused_computation.17 | convolution fusion | flops 1811939328 | bytes 9043968 | tf_op jit(solution)/shard_map/dot_general | solution.py:45
  102.0 0.0 copy-start.2
  102.0 2.2 reshape_reshape.4
  104.2 1.2 copy.20
  105.5 14.7 %all_to_all.34 = f32[4,32,1,4,384]{4,3,1,2,0:T(4,128)} all-to-all(f32[4,32,1,4,384]{4,3,1,2,0:T(4,128)S(1)} %bitcast.25), channel_id=1, replica_groups=mesh['groups'=2,'gx_0'=16,'gx_1'=2,'gy'=4] {'gy'}, dimensions={0} | all-to-all | bytes 1572864 | tf_op jit(solution)/shard_map/all_to_all | solution.py:20
  120.1 2.0 reduce_sum.18
  122.1 8.8 %all-to-all-start.1 = ((bf16[32,4,384]{2,1,0:T(4,128)(2,1)}), bf16[32,4,384]{2,1,0:T(4,128)(2,1)}, u32[]{:S(2)}, u32[]{:S(2)}) async-start(bf16[32,4,384]{2,1,0:T(4,128)(2,1)} %reduce_sum.18), calls=%async_computation.1 | async-start | bytes 196608 | tf_op jit(solution)/shard_map/all_to_all | solution.py:54
  130.9 0.1 reduce-scatter.3.cloned.1.call-start
  131.0 0.0 copy-done.2
  131.0 0.1 iota_compare_fusion
  131.1 15.0 %all-to-all-done.1 = bf16[32,4,384]{2,1,0:T(4,128)(2,1)} async-done(((bf16[32,4,384]{2,1,0:T(4,128)(2,1)}), bf16[32,4,384]{2,1,0:T(4,128)(2,1)}, u32[]{:S(2)}, u32[]{:S(2)}) %all-to-all-start.1) | async-done | bytes 98336 | tf_op jit(solution)/shard_map/all_to_all | solution.py:54
  146.1 1.5 copy.12
  147.6 1.6 reshape.48
  149.2 2.4 fusion.5
  151.6 0.0 copy-start.1
  151.6 0.9 copy-done.1
  152.5 0.3 fusion.9
  152.8 3.2 %convolution_convert_fusion = bf16[4,48,256]{2,1,0:T(8,128)(2,1)} fusion(bf16[4,1024,256]{2,1,0:T(8,128)(2,1)} %param.10, f32[4,48]{1,0:T(4,128)S(1)} %fusion.9, f32[4,48,1024]{2,1,0:T(8,128)} %copy-done.1, pred[4,1024]{1,0:T(4,128)(4,1)S(1)} %iota_compare_fusion), kind=kOutput, calls=%fused_computation.8 | convolution fusion | flops 101500096 | bytes 2986752 | tf_op jit(solution)/shard_map/bhl,bld->bhd/dot_general | solution.py:64
  156.0 1.6 all_to_all.28
  157.6 0.9 copy.13
  158.6 18.9 %all_to_all.35 = bf16[4,32,384]{2,0,1:T(4,128)(2,1)S(1)} all-to-all(bf16[4,32,384]{2,0,1:T(4,128)(2,1)S(1)} %copy.13), channel_id=1, replica_groups=mesh['groups'=2,'gx_0'=16,'gx_1'=2,'gy'=4] {'gx_0','gx_1'}, dimensions={1} | all-to-all | bytes 196608 | tf_op jit(solution)/shard_map/all_to_all | solution.py:66
  177.5 13.6 %all_gather.7 = bf16[32,16,384]{2,0,1:T(8,128)(2,1)S(1)} all-gather(bf16[32,4,384]{2,0,1:T(8,128)(2,1)S(1)} %copy.14), channel_id=1, replica_groups=mesh['groups'=2,'gx_0'=16,'gx_1'=2,'gy'=4] {'gy'}, dimensions={1}, use_global_device_ids=true | all-gather | bytes 491520 | tf_op jit(solution)/shard_map/all_gather | solution.py:68
  191.1 0.1 copy.15
  191.2 0.0 copy-done
  191.2 2.6 convolution_bitcast_fusion
  193.8 4.2 %copy.16 = f32[2,16,16,4608]{3,2,1,0:T(8,128)} copy(f32[2,16,16,4608]{3,2,0,1:T(8,128)S(1)} %convolution_bitcast_fusion) | data formatting | bytes 18874368 | tf_op jit(solution)/shard_map/transpose | solution.py:27
  198.1 0.1 reduce-scatter.3.cloned.1.call-update
  198.2 0.1 reduce-scatter.5.cloned.1.call-start
  198.2 17.6 %reduce-scatter.3.cloned.1.call-done = f32[16,16,4608]{2,1,0:T(8,128)} async-done(((f32[32,16,4608]{2,1,0:T(8,128)}), f32[16,16,4608]{2,1,0:T(8,128)}) %reduce-scatter.3.cloned.1.call-update) | async-done | bytes 4718608 | tf_op jit(solution)/shard_map/reduce_scatter | solution.py:30
  215.8 0.1 reduce-scatter.5.cloned.1.call-update
  215.9 84.3 %reduce-scatter.5.cloned.1.call-done = f32[1,16,4608]{2,1,0:T(8,128)} async-done(((f32[16,16,4608]{2,1,0:T(8,128)}), f32[1,16,4608]{2,1,0:T(8,128)}) %reduce-scatter.5.cloned.1.call-update) | async-done | bytes 294928 | tf_op jit(solution)/shard_map/reduce_scatter | solution.py:30
  300.2 1.6 convert_bitcast_fusion
  (1 shorter events, 0.0 us)
Async XLA Ops:
  6.5 184.7 %copy-start = (bf16[384,4608]{1,0:T(8,128)(2,1)S(1)}, bf16[384,4608]{1,0:T(8,128)(2,1)}, u32[]{:S(2)}) copy-start(bf16[384,4608]{1,0:T(8,128)(2,1)} %param.8) | copy-start | bytes 10616836
  6.6 88.5 %all-gather.2.cloned.1.call-start = ((), (), s32[]{:S(2)}) async-start(), calls=%async_computation.5 | async-start | bytes 4866048 | tf_op jit(solution)/shard_map/all_gather | solution.py:46
  102.0 29.0 %copy-start.2 = (s32[4]{0:T(128)S(1)}, s32[4]{0:T(128)}, u32[]{:S(2)}) copy-start(s32[4]{0:T(128)} %param.11) | copy-start | bytes 52
  122.1 24.0 %all-to-all-start.1 = ((bf16[32,4,384]{2,1,0:T(4,128)(2,1)}), bf16[32,4,384]{2,1,0:T(4,128)(2,1)}, u32[]{:S(2)}, u32[]{:S(2)}) async-start(bf16[32,4,384]{2,1,0:T(4,128)(2,1)} %reduce_sum.18), calls=%async_computation.1 | async-start | bytes 196608 | tf_op jit(solution)/shard_map/all_to_all | solution.py:54
  130.9 84.9 %reduce-scatter.3.cloned.1.call-start = ((), (), s32[]{:S(2)}) async-start(), calls=%async_computation.6 | async-start | bytes 14155776 | tf_op jit(solution)/shard_map/reduce_scatter | solution.py:30
  151.6 0.9 copy-start.1
  198.2 102.1 %reduce-scatter.5.cloned.1.call-start = ((), (), s32[]{:S(2)}) async-start(), calls=%async_computation.7 | async-start | bytes 5013504 | tf_op jit(solution)/shard_map/reduce_scatter | solution.py:30
Sparse Core Ops, SparseCore 0:
  9.2 85.8 all-gather.1
  198.3 17.4 reduce-scatter.2
  218.4 81.7 reduce-scatter.4
where the time goes:
time: 309 us; the launch traced here: 308 us
  waiting for transfers between devices  206 us (67%)
  blocking collectives  47.2 us (15%)
  matrix products  15.2 us (5%)
  local copies, waits for them, and re-layouts  14.4 us (5%)
  between operations  13.2 us (4%)
  starting transfers between devices  8.93 us (3%)
  other arithmetic  3.99 us (1%)
    reduce_scatter x2, waiting for transfers between devices, reduced_to_own(): tiles = lax.psum_scatter(tiles, axes[k], scatter_dimension=0, tiled=True)  102 us
    all_gather x1, waiting for transfers between devices, body(): lax.all_gather(hidden_in, GX, axis=0, tiled=True)  87.8 us
    all_to_all x1, blocking collectives, body(): lax.all_to_all(attended, GX, split_axis=1, concat_axis=0, tiled=True)  18.9 us
    all_to_all x1, waiting for transfers between devices, body(): lax.all_to_all(query_rows, GX, split_axis=0, concat_axis=1, tiled=True)  15 us
    all_to_all x1, blocking collectives, summed_on_arrival(): tiles = lax.all_to_all(cut_along(x, dim, size), axis, 0, 0, tiled=True)  14.7 us
    all_gather x1, blocking collectives, body(): gathered = lax.all_gather(stacked, 'gy', axis=1, tiled=True)  13.6 us
    all_to_all x1, starting transfers between devices, body(): lax.all_to_all(query_rows, GX, split_axis=0, concat_axis=1, tiled=True)  8.8 us
    dot_general x1, matrix products, body(): jnp.dot(lax.all_gather(hidden_in, GX, axis=0, tiled=True), w_query, prefe...  6.93 us
  transfers between devices with their start and end apart: 4, of which 4 were waited for; matrix products, arithmetic and copies ran while one was open for 0% of the time, Pallas kernels for 0%

commit v1 on v0

v1 whole, which is shorter than its diff:
```python
import functools

import jax
import jax.numpy as jnp
from jax import lax
from jax.experimental import pallas as pl
from jax.experimental.pallas import tpu as pltpu
from jax.sharding import PartitionSpec as P

MESH = pl.DeviceIdType.MESH
CORES = 2
IN_CHUNKS = 4
OUT_CHUNKS = 6
F32 = jnp.float32
BF16 = jnp.bfloat16


def source_offset(u, half):
    return half - (u + 1) // 2 if u % 2 else half + u // 2


def kernel(
    nz,
    nx,
    lengths,
    hidden,
    w_query,
    w_out,
    keys,
    values,
    out,
    gathered,
    wq,
    wo,
    k_buf,
    v_buf,
    acc,
    part,
    part_in,
    q_send,
    q_in,
    q_wide,
    att_wide,
    att_send,
    att_in,
    att,
    sums,
    sums_in,
    last,
    local_sem,
    ring_send_sem,
    ring_sem,
    pair_send_sem,
    pair_sem,
    part_send_sem,
    part_sem,
    q_send_sem,
    q_sem,
    att_send_sem,
    att_sem,
    rows_send_sem,
    rows_sem,
    swap_send_sem,
    swap_sem,
    wo_send_sem,
    wo_sem,
    sums_send_sem,
    sums_sem,
    last_send_sem,
    last_sem,
):
    half = nz // 2
    gx = lax.axis_index("gx")
    x = lax.axis_index("gy")
    z = gx // CORES
    c = gx % CORES
    other = 1 - c
    seqs, slots, hd = k_buf.shape
    width = hidden.shape[1]
    cols = width // IN_CHUNKS
    own_cols = width // CORES
    out_cols = own_cols // OUT_CHUNKS
    feats = w_query.shape[1]
    block = nx * seqs

    def at_z(chip, core):
        return {"gx": lax.rem(chip + 2 * nz, nz) * CORES + core}

    def at_x(offset):
        return {"gy": lax.rem(x + offset, nx)}

    side = (at_z(z + 1, c), at_z(z - 1, c))
    pair = {"gx": z * CORES + other}

    def remote(src, dst, send_sem, recv_sem, device):
        return pltpu.make_async_remote_copy(
            src_ref=src, dst_ref=dst, send_sem=send_sem, recv_sem=recv_sem, device_id=device, device_id_type=MESH
        )

    def half_cols(core):
        return pl.ds(pl.multiple_of(core * own_cols, 128), own_cols)

    own_slot = gathered.at[half - 1, CORES + c]
    loads = [
        pltpu.make_async_copy(hidden, own_slot, local_sem.at[0]),
        pltpu.make_async_copy(w_query, wq, local_sem.at[1]),
        pltpu.make_async_copy(w_out.at[:, half_cols(c)], wo.at[c], local_sem.at[2]),
        pltpu.make_async_copy(keys, k_buf, local_sem.at[3]),
        pltpu.make_async_copy(values, v_buf, local_sem.at[4]),
    ]
    loads[0].start()
    loads[1].start()

    barrier = pltpu.get_barrier_semaphore()
    greeted = [*side, pair] + [at_x(k) for k in range(1, nx)]
    for device in greeted:
        pl.semaphore_signal(barrier, inc=1, device_id=device, device_id_type=MESH)
    pl.semaphore_wait(barrier, len(greeted))
    loads[0].wait()

    def piece(j):
        return pl.ds(j * cols, cols)

    def home(s, d):
        return 0 if isinstance(s, int) and s == half - 1 else d

    def ring(d, s, j):
        src = own_slot if isinstance(s, int) and s == 0 else gathered.at[s - 1, CORES * d + c]
        dst = gathered.at[s, CORES * home(s, d) + c]
        return remote(src.at[:, piece(j)], dst.at[:, piece(j)], ring_send_sem.at[d, s], ring_sem.at[d, s, j], side[d])

    def to_pair(d, s, j):
        ref = gathered.at[s, CORES * home(s, d) + c, :, piece(j)]
        return remote(ref, ref, pair_send_sem.at[home(s, d), s], pair_sem.at[home(s, d), s], pair)

    def travels(d, s, j):
        return s < half - 1 or (j < IN_CHUNKS // 2) == (d == 0)

    def dot_piece(s, j):
        if j == 0:
            for d in range(2):
                ref = gathered.at[s, CORES * d + other]
                remote(ref, ref, pair_send_sem.at[d, s], pair_sem.at[d, s], pair).wait_recv()
        lhs = gathered[s, :, :, j * cols : (j + 1) * cols].reshape(2 * CORES * block, cols)
        term = jnp.dot(lhs, wq[j * cols : (j + 1) * cols, :], preferred_element_type=F32)
        if j == 0:
            acc[...] = term
        else:
            acc[...] += term

    def send_parts(s):
        for g in range(nx):
            part[s, g] = jnp.concatenate(
                [acc[b * block + g * seqs : b * block + (g + 1) * seqs, :] for b in range(2 * CORES)], axis=0
            )
        for k in range(1, nx):
            part_copy(s, k).start()

    def part_copy(s, k):
        return remote(
            part.at[s, lax.rem(x + k, nx)], part_in.at[s, k - 1], part_send_sem.at[s, k - 1], part_sem.at[s, k - 1], at_x(k)
        )

    def q_copy(s, d, r):
        core = lax.rem(c + r, CORES)
        if isinstance(s, int) and s == half - 1:
            chip = z + half if d == 0 else z
        else:
            chip = z - 1 - s if d == 0 else z + 1 + s
        return remote(q_send.at[s, CORES * d + core], q_in.at[gx], q_send_sem, q_sem.at[gx], at_z(chip, core))

    def send_queries(s):
        total = part[s, x]
        for k in range(1, nx):
            part_copy(s, k).wait_recv()
            total = total + part_in[s, k - 1]
        for b in range(2 * CORES):
            q_send[s, b] = total[b * seqs : (b + 1) * seqs, :].astype(BF16)
        for d in range(2):
            for r in range(CORES):
                if isinstance(s, int) and s == half - 1 and d == 1 and r == 0:
                    q_in[gx] = q_send[s, CORES + c]
                else:
                    q_copy(s, d, r).start()

    for j in range(IN_CHUNKS):
        for d in range(2):
            if travels(d, 0, j):
                ring(d, 0, j).start()
    for j in range(IN_CHUNKS):
        ref = own_slot.at[:, piece(j)]
        remote(ref, ref, pair_send_sem.at[1, half - 1], pair_sem.at[1, half - 1], pair).start()
    loads[1].wait()
    for load in loads[2:]:
        load.start()
    wo_copy = remote(w_out.at[:, half_cols(other)], wo.at[c], wo_send_sem, wo_sem, pair)
    wo_copy.start()

    def gather_step(s):
        known = isinstance(s, int)
        for j in range(IN_CHUNKS):
            for d in range(2):
                if not known or travels(d, s, j):
                    ring(d, s, j).wait_recv()
                    if not known or (s < half - 1 and travels(d, s + 1, j)):
                        ring(d, s + 1, j).start()
                    to_pair(d, s, j).start()
            if known:
                if s >= 1:
                    dot_piece(s - 1, j)
            else:
                pl.when(s >= 1)(functools.partial(dot_piece, s - 1, j))
        if known:
            if s >= 1:
                send_parts(s - 1)
            if s >= 2:
                send_queries(s - 2)
        else:
            pl.when(s >= 1)(functools.partial(send_parts, s - 1))
            pl.when(s >= 2)(functools.partial(send_queries, s - 2))

    gather_step(0)

    @pl.loop(1, half - 2)
    def _(s):
        gather_step(s)

    for s in range(max(half - 2, 1), half):
        gather_step(s)
    for j in range(IN_CHUNKS):
        dot_piece(half - 1, j)
    send_parts(half - 1)
    send_queries(half - 2)
    send_queries(half - 1)

    for load in loads[3:]:
        load.wait()

    @pl.loop(1, nz * CORES)
    def _(k):
        ref = q_in.at[lax.rem(gx + k, nz * CORES)]
        remote(ref, ref, q_send_sem, q_sem.at[lax.rem(gx + k, nz * CORES)], pair).wait_recv()

    q_wide[...] = q_in[...].reshape(nz, CORES, seqs, feats).astype(F32)
    heads = CORES * feats // hd
    for i in range(seqs):
        rows = jnp.concatenate([q_wide[:, core, i, :] for core in range(CORES)], axis=1)
        query = jnp.concatenate([rows[:, h * hd : (h + 1) * hd] for h in range(heads)], axis=0).astype(BF16)
        scores = lax.dot_general(query, k_buf[i], (((1,), (1,)), ((), ())), preferred_element_type=F32)
        scores = scores * F32(hd**-0.5)
        live = lax.broadcasted_iota(jnp.int32, scores.shape, 1) < lengths[i]
        scores = jnp.where(live, scores, F32(-1e30))
        expo = jnp.where(live, jnp.exp(scores - jnp.max(scores, axis=1, keepdims=True)), F32(0.0))
        probs = (expo / jnp.sum(expo, axis=1, keepdims=True)).astype(BF16)
        mixed = jnp.dot(probs, v_buf[i], preferred_element_type=F32)
        wide = jnp.concatenate([mixed[h * nz : (h + 1) * nz, :] for h in range(heads)], axis=1)
        for core in range(CORES):
            att_wide[:, core, i, :] = wide[:, core * feats : (core + 1) * feats]
    att_send[...] = att_wide[...].astype(BF16)

    def att_copy(u, r):
        core = lax.rem(c + r, CORES)
        chip = lax.rem(z - source_offset(u, half) + nz, nz)
        return remote(att_send.at[chip, core], att_in.at[x, u, c], att_send_sem, att_sem.at[u, c], at_z(chip, core))

    for u in range(nz):
        for r in range(CORES):
            if u == nz - 1 and r == 0:
                att_in[x, u, c] = att_send[z, c]
            else:
                att_copy(u, r).start()

    per = nz // 4
    batches = [(b * per, (b + 1) * per) for b in range(4)]

    def rows_copy(b, k):
        ref = att_in.at[x, batches[b][0] : batches[b][1]]
        return remote(ref, ref, rows_send_sem.at[b, k - 1], rows_sem.at[b, k - 1], at_x(k))

    def swap_copy(b):
        ref = att.at[c, batches[b][0] : batches[b][1]]
        return remote(ref, ref, swap_send_sem.at[b], swap_sem.at[b], pair)

    for b in range(4):
        for u in range(*batches[b]):
            for r in range(CORES):
                core = lax.rem(c + r, CORES)
                if u < nz - 1 or r > 0:
                    ref = att_in.at[x, u, core]
                    remote(ref, ref, att_send_sem, att_sem.at[u, core], pair).wait_recv()
        for k in range(1, nx):
            rows_copy(b, k).start()
    for b in range(4):
        for k in range(1, nx):
            rows_copy(b, k).wait_recv()
        for u in range(*batches[b]):
            for core in range(CORES):
                att[c, u, core] = jnp.concatenate(
                    [att_in[g, u, core].astype(F32) for g in range(nx)], axis=0
                ).astype(BF16)
        swap_copy(b).start()
    loads[2].wait()
    wo_copy.wait_recv()
    for b in range(4):
        swap_copy(b).wait_recv()

    def out_piece(j):
        return pl.ds(j * out_cols, out_cols)

    def projected(u, count, j):
        lhs = jnp.concatenate(
            [att[f, pl.ds(u, count)].reshape(count * CORES * block, feats) for f in range(CORES)], axis=1
        )
        rhs = wo[:, :, j * out_cols : (j + 1) * out_cols].reshape(CORES * feats, out_cols)
        return jnp.dot(lhs, rhs, preferred_element_type=F32)

    def sums_copy(d, s, j):
        return remote(
            sums.at[d, s, :, out_piece(j)],
            sums_in.at[d, s, :, out_piece(j)],
            sums_send_sem.at[d, s],
            sums_sem.at[d, s, j],
            side[d],
        )

    def starts(d, j):
        return (j < OUT_CHUNKS // 2) == (d == 0)

    tall = CORES * block

    def out_step(s):
        known = isinstance(s, int)
        for j in range(OUT_CHUNKS):
            span = slice(j * out_cols, (j + 1) * out_cols)
            if known and s == 0:
                d = 0 if starts(0, j) else 1
                sums[d, 0, :, span] = projected(0, 1, j).astype(BF16)
                sums_copy(d, 0, j).start()
                continue
            both = projected(2 * s - 1, 2, j)
            for d in range(2):
                term = both[d * tall : (d + 1) * tall]
                if not known or s > 1 or starts(d, j):
                    sums_copy(d, s - 1, j).wait_recv()
                    term = term + sums_in[d, s - 1, :, span].astype(F32)
                sums[d, s, :, span] = term.astype(BF16)
                sums_copy(d, s, j).start()

    out_step(0)
    out_step(1)

    @pl.loop(2, half)
    def _(s):
        out_step(s)

    def last_copy(j):
        own = pl.ds(pl.multiple_of(c * own_cols + j * out_cols, 128), out_cols)
        return remote(
            last.at[other, :, out_piece(j)], out.at[:, own], last_send_sem.at[j], last_sem.at[j], pair
        )

    for j in range(OUT_CHUNKS):
        span = slice(j * out_cols, (j + 1) * out_cols)
        term = projected(nz - 1, 1, j)
        for d in range(2):
            sums_copy(d, half - 1, j).wait_recv()
            term = term + sums_in[d, half - 1, :, span].astype(F32)
        for core in range(CORES):
            last[core, :, span] = term[core * block : (core + 1) * block].astype(BF16)
        last_copy(j).start()
    out[:, half_cols(c)] = last[c]
    for j in range(OUT_CHUNKS):
        last_copy(j).wait_recv()

    def ring_sent(d, s, whole):
        ref = gathered.at[0, c] if whole else gathered.at[0, c, :, pl.ds(0, width // 2)]
        remote(ref, ref, ring_send_sem.at[d, s], ring_sem.at[d, s, 0], side[d]).wait_send()

    def pair_sent(d, s):
        ref = gathered.at[0, c]
        remote(ref, ref, pair_send_sem.at[d, s], pair_sem.at[d, s], pair).wait_send()

    @pl.loop(0, half)
    def _(s):
        for d in range(2):
            pair_sent(d, s)
        for k in range(1, nx):
            part_copy(s, k).wait_send()

    @pl.loop(0, half - 1)
    def _(s):
        for d in range(2):
            ring_sent(d, s, True)

    @pl.loop(1, half)
    def _(s):
        for d in range(2):
            ref = sums.at[d, s]
            remote(ref, ref, sums_send_sem.at[d, s], sums_sem.at[d, s, 0], side[d]).wait_send()

    for d in range(2):
        ring_sent(d, half - 1, False)
        ref = sums.at[d, 0, :, pl.ds(0, own_cols // 2)]
        remote(ref, ref, sums_send_sem.at[d, 0], sums_sem.at[d, 0, 0], side[d]).wait_send()
    ref = q_in.at[pl.ds(0, nz * CORES - 1)]
    remote(ref, ref, q_send_sem, q_sem.at[0], pair).wait_send()
    remote(ref, ref, att_send_sem, att_sem.at[0, 0], pair).wait_send()
    for b in range(4):
        swap_copy(b).wait_send()
        for k in range(1, nx):
            rows_copy(b, k).wait_send()
    wo_copy.wait_send()
    for j in range(OUT_CHUNKS):
        last_copy(j).wait_send()


def solution(mesh):
    nz = mesh.shape["gx"] // CORES
    nx = mesh.shape["gy"]
    half = nz // 2

    def body(hidden_in, w_query, w_out, cache_keys, cache_values, lengths):
        block, width = hidden_in.shape
        feats = w_query.shape[1]
        seqs, slots, hd = cache_keys.shape
        own_cols = width // CORES
        dma = pltpu.SemaphoreType.DMA
        hbm = pl.BlockSpec(memory_space=pltpu.HBM)
        return pl.pallas_call(
            functools.partial(kernel, nz, nx),
            out_shape=jax.ShapeDtypeStruct((block, width), BF16),
            in_specs=[pl.BlockSpec(memory_space=pltpu.SMEM)] + [hbm] * 5,
            out_specs=pl.BlockSpec(memory_space=pltpu.VMEM),
            scratch_shapes=[
                pltpu.VMEM((half, 2 * CORES, block, width), BF16),
                pltpu.VMEM(w_query.shape, BF16),
                pltpu.VMEM((CORES, feats, own_cols), BF16),
                pltpu.VMEM(cache_keys.shape, BF16),
                pltpu.VMEM(cache_values.shape, BF16),
                pltpu.VMEM((2 * CORES * block, feats), F32),
                pltpu.VMEM((half, nx, 2 * CORES * seqs, feats), F32),
                pltpu.VMEM((half, nx - 1, 2 * CORES * seqs, feats), F32),
                pltpu.VMEM((half, 2 * CORES, seqs, feats), BF16),
                pltpu.VMEM((nz * CORES, seqs, feats), BF16),
                pltpu.VMEM((nz, CORES, seqs, feats), F32),
                pltpu.VMEM((nz, CORES, seqs, feats), F32),
                pltpu.VMEM((nz, CORES, seqs, feats), BF16),
                pltpu.VMEM((nx, nz, CORES, seqs, feats), BF16),
                pltpu.VMEM((CORES, nz, CORES, block, feats), BF16),
                pltpu.VMEM((2, half, CORES * block, own_cols), BF16),
                pltpu.VMEM((2, half, CORES * block, own_cols), BF16),
                pltpu.VMEM((CORES, block, own_cols), BF16),
                dma((5,)),
                dma((2, half)),
                dma((2, half, IN_CHUNKS)),
                dma((2, half)),
                dma((2, half)),
                dma((half, nx - 1)),
                dma((half, nx - 1)),
                dma(()),
                dma((nz * CORES,)),
                dma(()),
                dma((nz, CORES)),
                dma((4, nx - 1)),
                dma((4, nx - 1)),
                dma((4,)),
                dma((4,)),
                dma(()),
                dma(()),
                dma((2, half)),
                dma((2, half, OUT_CHUNKS)),
                dma((OUT_CHUNKS,)),
                dma((OUT_CHUNKS,)),
            ],
            compiler_params=pltpu.CompilerParams(
                collective_id=0, has_side_effects=True, vmem_limit_bytes=60 * 2**20
            ),
            name="decode_step",
        )(lengths, hidden_in, w_query, w_out, cache_keys, cache_values)

    return jax.shard_map(
        body,
        mesh=mesh,
        in_specs=(
            P(("groups", "gx"), "gy"),
            P("gy", "gx"),
            P("gx", "gy"),
            P(("groups", "gx", "gy"), None, None),
            P(("groups", "gx", "gy"), None, None),
            P(("groups", "gx", "gy")),
        ),
        out_specs=P(("groups", "gx"), "gy"),
        check_vma=False,
    )
```

time: 309 us -> 125 us (0.40)
  the two profiles are of different devices: /device:TPU:36 before, /device:TPU:33 now
where the time goes in v1:
time: 125 us
  Pallas kernels  123 us (98%)
  local copies, waits for them, and re-layouts  1.58 us (1%)
    pallas_call x1, Pallas kernels, body(): pl.pallas_call(functools.partial(kernel, nz, nx), out_shape=jax.ShapeDtyp...  123 us

profile of v1, /device:TPU:33, one launch (start us, length us, event | category | flops | bytes accessed | tf_op | source)
XLA Modules:
  0.0 124.7 jit_solution(6203218680298589176)
XLA Ops:
  0.0 123.1 %decode_step.1 = bf16[16,4608]{1,0:T(8,128)(2,1)} custom-call(s32[4]{0:T(128)} %lengths.1, bf16[16,4608]{1,0:T(8,128)(2,1)} %hidden.1, bf16[4608,384]{1,0:T(8,128)(2,1)} %w_query.1, bf16[384,4608]{1,0:T(8,128)(2,1)} %w_out.1, bf16[4,1024,256]{2,1,0:T(8,128)(2,1)} %keys.1, bf16[4,1024,256]{2,1,0:T(8,128)(2,1)} %values.1), custom_call_target="tpu_custom_call" | custom-call | tf_op jit(solution)/shard_map/decode_step/pallas_call | solution.py:429
  123.1 1.6 %copy.8 = bf16[16,4608]{1,0:T(8,128)(2,1)} copy(bf16[16,4608]{1,0:T(8,128)(2,1)} %decode_step.1) | data formatting | bytes 294912

commit v2 on v1

--- a/solution.py
+++ b/solution.py
@@ -9,14 +9,15 @@
 
 MESH = pl.DeviceIdType.MESH
 CORES = 2
-IN_CHUNKS = 4
-OUT_CHUNKS = 6
+IN_CHUNKS = 6
+OUT_CHUNKS = 9
+PER_BATCH = 4
 F32 = jnp.float32
 BF16 = jnp.bfloat16
 
 
-def source_offset(u, half):
-    return half - (u + 1) // 2 if u % 2 else half + u // 2
+def source_offset(v, half):
+    return 0 if v == 0 else half + v // 2 if v % 2 else half - v // 2
 
 
 def kernel(
@@ -100,7 +101,7 @@
     def half_cols(core):
         return pl.ds(pl.multiple_of(core * own_cols, 128), own_cols)
 
-    own_slot = gathered.at[half - 1, CORES + c]
+    own_slot = gathered.at[half, c]
     loads = [
         pltpu.make_async_copy(hidden, own_slot, local_sem.at[0]),
         pltpu.make_async_copy(w_query, wq, local_sem.at[1]),
@@ -136,61 +137,69 @@
     def travels(d, s, j):
         return s < half - 1 or (j < IN_CHUNKS // 2) == (d == 0)
 
-    def dot_piece(s, j):
+    def blocks(t):
+        return CORES if isinstance(t, int) and t >= half - 1 else 2 * CORES
+
+    def dot_piece(t, j):
         if j == 0:
-            for d in range(2):
-                ref = gathered.at[s, CORES * d + other]
-                remote(ref, ref, pair_send_sem.at[d, s], pair_sem.at[d, s], pair).wait_recv()
-        lhs = gathered[s, :, :, j * cols : (j + 1) * cols].reshape(2 * CORES * block, cols)
+            for d in range(blocks(t) // CORES):
+                ref = gathered.at[t, CORES * d + other]
+                remote(ref, ref, pair_send_sem.at[d, t], pair_sem.at[d, t], pair).wait_recv()
+        tall = blocks(t) * block
+        lhs = gathered[t, : blocks(t), :, j * cols : (j + 1) * cols].reshape(tall, cols)
         term = jnp.dot(lhs, wq[j * cols : (j + 1) * cols, :], preferred_element_type=F32)
         if j == 0:
-            acc[...] = term
+            acc[:tall] = term
         else:
-            acc[...] += term
-
-    def send_parts(s):
+            acc[:tall] += term
+
+    def part_copy(t, k):
+        rows = pl.ds(0, blocks(t) * seqs)
+        return remote(
+            part.at[t, lax.rem(x + k, nx), rows],
+            part_in.at[t, k - 1, rows],
+            part_send_sem.at[t, k - 1],
+            part_sem.at[t, k - 1],
+            at_x(k),
+        )
+
+    def send_parts(t):
         for g in range(nx):
-            part[s, g] = jnp.concatenate(
-                [acc[b * block + g * seqs : b * block + (g + 1) * seqs, :] for b in range(2 * CORES)], axis=0
+            part[t, g, : blocks(t) * seqs] = jnp.concatenate(
+                [acc[b * block + g * seqs : b * block + (g + 1) * seqs, :] for b in range(blocks(t))], axis=0
             )
         for k in range(1, nx):
-            part_copy(s, k).start()
-
-    def part_copy(s, k):
-        return remote(
-            part.at[s, lax.rem(x + k, nx)], part_in.at[s, k - 1], part_send_sem.at[s, k - 1], part_sem.at[s, k - 1], at_x(k)
-        )
-
-    def q_copy(s, d, r):
+            part_copy(t, k).start()
+
+    def q_copy(t, d, r):
         core = lax.rem(c + r, CORES)
-        if isinstance(s, int) and s == half - 1:
-            chip = z + half if d == 0 else z
+        if isinstance(t, int) and t >= half - 1:
+            chip = z if t == half else z + half
         else:
-            chip = z - 1 - s if d == 0 else z + 1 + s
-        return remote(q_send.at[s, CORES * d + core], q_in.at[gx], q_send_sem, q_sem.at[gx], at_z(chip, core))
-
-    def send_queries(s):
-        total = part[s, x]
-        for k in range(1, nx):
-            part_copy(s, k).wait_recv()
-            total = total + part_in[s, k - 1]
-        for b in range(2 * CORES):
-            q_send[s, b] = total[b * seqs : (b + 1) * seqs, :].astype(BF16)
-        for d in range(2):
+            chip = z - 1 - t if d == 0 else z + 1 + t
+        return remote(q_send.at[t, CORES * d + core], q_in.at[gx], q_send_sem, q_sem.at[gx], at_z(chip, core))
+
+    def send_queries(t):
+        rows = blocks(t) * seqs
+        total = part[t, x, :rows]
+        for k in range(1, nx):
+            part_copy(t, k).wait_recv()
+            total = total + part_in[t, k - 1, :rows]
+        for b in range(blocks(t)):
+            q_send[t, b] = total[b * seqs : (b + 1) * seqs, :].astype(BF16)
+        for d in range(blocks(t) // CORES):
             for r in range(CORES):
-                if isinstance(s, int) and s == half - 1 and d == 1 and r == 0:
-                    q_in[gx] = q_send[s, CORES + c]
+                if isinstance(t, int) and t == half and r == 0:
+                    q_in[gx] = q_send[half, c]
                 else:
-                    q_copy(s, d, r).start()
+                    q_copy(t, d, r).start()
 
     for j in range(IN_CHUNKS):
         for d in range(2):
-            if travels(d, 0, j):
-                ring(d, 0, j).start()
+            ring(d, 0, j).start()
     for j in range(IN_CHUNKS):
         ref = own_slot.at[:, piece(j)]
-        remote(ref, ref, pair_send_sem.at[1, half - 1], pair_sem.at[1, half - 1], pair).start()
-    loads[1].wait()
+        remote(ref, ref, pair_send_sem.at[0, half], pair_sem.at[0, half], pair).start()
     for load in loads[2:]:
         load.start()
     wo_copy = remote(w_out.at[:, half_cols(other)], wo.at[c], wo_send_sem, wo_sem, pair)
@@ -198,6 +207,7 @@
 
     def gather_step(s):
         known = isinstance(s, int)
+        before = half if known and s == 0 else s - 1
         for j in range(IN_CHUNKS):
             for d in range(2):
                 if not known or travels(d, s, j):
@@ -205,27 +215,21 @@
                     if not known or (s < half - 1 and travels(d, s + 1, j)):
                         ring(d, s + 1, j).start()
                     to_pair(d, s, j).start()
-            if known:
-                if s >= 1:
-                    dot_piece(s - 1, j)
-            else:
-                pl.when(s >= 1)(functools.partial(dot_piece, s - 1, j))
-        if known:
-            if s >= 1:
-                send_parts(s - 1)
-            if s >= 2:
-                send_queries(s - 2)
-        else:
-            pl.when(s >= 1)(functools.partial(send_parts, s - 1))
-            pl.when(s >= 2)(functools.partial(send_queries, s - 2))
+            if known and s == 0 and j == 0:
+                loads[1].wait()
+            dot_piece(before, j)
+        send_parts(before)
+        if not known or s > 0:
+            send_queries(half if known and s == 1 else s - 2)
 
     gather_step(0)
-
-    @pl.loop(1, half - 2)
+    gather_step(1)
+
+    @pl.loop(2, half - 2)
     def _(s):
         gather_step(s)
 
-    for s in range(max(half - 2, 1), half):
+    for s in range(max(half - 2, 2), half):
         gather_step(s)
     for j in range(IN_CHUNKS):
         dot_piece(half - 1, j)
@@ -258,58 +262,63 @@
             att_wide[:, core, i, :] = wide[:, core * feats : (core + 1) * feats]
     att_send[...] = att_wide[...].astype(BF16)
 
-    def att_copy(u, r):
+    def att_copy(v, r):
         core = lax.rem(c + r, CORES)
-        chip = lax.rem(z - source_offset(u, half) + nz, nz)
-        return remote(att_send.at[chip, core], att_in.at[x, u, c], att_send_sem, att_sem.at[u, c], at_z(chip, core))
-
-    for u in range(nz):
+        chip = z - source_offset(v, half)
+        return remote(
+            att_send.at[lax.rem(chip + nz, nz), core], att_in.at[x, v, c], att_send_sem, att_sem.at[v, c], at_z(chip, core)
+        )
+
+    for v in [*range(1, nz), 0]:
         for r in range(CORES):
-            if u == nz - 1 and r == 0:
-                att_in[x, u, c] = att_send[z, c]
+            if v == 0 and r == 0:
+                att_in[x, v, c] = att_send[z, c]
             else:
-                att_copy(u, r).start()
-
-    per = nz // 4
-    batches = [(b * per, (b + 1) * per) for b in range(4)]
+                att_copy(v, r).start()
+
+    batches = nz // PER_BATCH
+
+    def batch(b):
+        return pl.ds(b * PER_BATCH, PER_BATCH)
 
     def rows_copy(b, k):
-        ref = att_in.at[x, batches[b][0] : batches[b][1]]
+        ref = att_in.at[x, batch(b)]
         return remote(ref, ref, rows_send_sem.at[b, k - 1], rows_sem.at[b, k - 1], at_x(k))
 
     def swap_copy(b):
-        ref = att.at[c, batches[b][0] : batches[b][1]]
+        ref = att.at[c, batch(b)]
         return remote(ref, ref, swap_send_sem.at[b], swap_sem.at[b], pair)
 
-    for b in range(4):
-        for u in range(*batches[b]):
+    def pass_on(b):
+        for k in range(1, nx):
+            rows_copy(b, k).wait_recv()
+        for n in range(PER_BATCH):
+            for core in range(CORES):
+                v = b * PER_BATCH + n
+                att[c, v, core] = jnp.concatenate(
+                    [att_in[g, v, core].astype(F32) for g in range(nx)], axis=0
+                ).astype(BF16)
+        swap_copy(b).start()
+
+    for b in range(batches):
+        for v in range(b * PER_BATCH, (b + 1) * PER_BATCH):
             for r in range(CORES):
                 core = lax.rem(c + r, CORES)
-                if u < nz - 1 or r > 0:
-                    ref = att_in.at[x, u, core]
-                    remote(ref, ref, att_send_sem, att_sem.at[u, core], pair).wait_recv()
+                if v > 0 or r > 0:
+                    ref = att_in.at[x, v, core]
+                    remote(ref, ref, att_send_sem, att_sem.at[v, core], pair).wait_recv()
         for k in range(1, nx):
             rows_copy(b, k).start()
-    for b in range(4):
-        for k in range(1, nx):
-            rows_copy(b, k).wait_recv()
-        for u in range(*batches[b]):
-            for core in range(CORES):
-                att[c, u, core] = jnp.concatenate(
-                    [att_in[g, u, core].astype(F32) for g in range(nx)], axis=0
-                ).astype(BF16)
-        swap_copy(b).start()
+    pass_on(0)
     loads[2].wait()
     wo_copy.wait_recv()
-    for b in range(4):
-        swap_copy(b).wait_recv()
 
     def out_piece(j):
         return pl.ds(j * out_cols, out_cols)
 
-    def projected(u, count, j):
+    def projected(v, count, j):
         lhs = jnp.concatenate(
-            [att[f, pl.ds(u, count)].reshape(count * CORES * block, feats) for f in range(CORES)], axis=1
+            [att[f, pl.ds(v, count)].reshape(count * CORES * block, feats) for f in range(CORES)], axis=1
         )
         rhs = wo[:, :, j * out_cols : (j + 1) * out_cols].reshape(CORES * feats, out_cols)
         return jnp.dot(lhs, rhs, preferred_element_type=F32)
@@ -324,7 +333,7 @@
         )
 
     def starts(d, j):
-        return (j < OUT_CHUNKS // 2) == (d == 0)
+        return (j < (OUT_CHUNKS + 1) // 2) == (d == 0)
 
     tall = CORES * block
 
@@ -334,10 +343,10 @@
             span = slice(j * out_cols, (j + 1) * out_cols)
             if known and s == 0:
                 d = 0 if starts(0, j) else 1
-                sums[d, 0, :, span] = projected(0, 1, j).astype(BF16)
+                sums[d, 0, :, span] = projected(1, 1, j).astype(BF16)
                 sums_copy(d, 0, j).start()
                 continue
-            both = projected(2 * s - 1, 2, j)
+            both = projected(2 * s, 2, j)
             for d in range(2):
                 term = both[d * tall : (d + 1) * tall]
                 if not known or s > 1 or starts(d, j):
@@ -346,10 +355,21 @@
                 sums[d, s, :, span] = term.astype(BF16)
                 sums_copy(d, s, j).start()
 
+    pass_on(1)
+    swap_copy(0).wait_recv()
     out_step(0)
     out_step(1)
 
-    @pl.loop(2, half)
+    @pl.loop(1, batches - 1)
+    def _(b):
+        pass_on(b + 1)
+        swap_copy(b).wait_recv()
+        out_step(2 * b)
+        out_step(2 * b + 1)
+
+    swap_copy(batches - 1).wait_recv()
+
+    @pl.loop(half - 2, half)
     def _(s):
         out_step(s)
 
@@ -361,7 +381,7 @@
 
     for j in range(OUT_CHUNKS):
         span = slice(j * out_cols, (j + 1) * out_cols)
-        term = projected(nz - 1, 1, j)
+        term = projected(0, 1, j)
         for d in range(2):
             sums_copy(d, half - 1, j).wait_recv()
             term = term + sums_in[d, half - 1, :, span].astype(F32)
@@ -372,40 +392,37 @@
     for j in range(OUT_CHUNKS):
         last_copy(j).wait_recv()
 
-    def ring_sent(d, s, whole):
-        ref = gathered.at[0, c] if whole else gathered.at[0, c, :, pl.ds(0, width // 2)]
-        remote(ref, ref, ring_send_sem.at[d, s], ring_sem.at[d, s, 0], side[d]).wait_send()
-
-    def pair_sent(d, s):
-        ref = gathered.at[0, c]
-        remote(ref, ref, pair_send_sem.at[d, s], pair_sem.at[d, s], pair).wait_send()
-
-    @pl.loop(0, half)
-    def _(s):
+    def left(ref, sem, recv_sem, device):
+        remote(ref, ref, sem, recv_sem, device).wait_send()
+
+    @pl.loop(0, half - 1)
+    def _(t):
         for d in range(2):
-            pair_sent(d, s)
-        for k in range(1, nx):
-            part_copy(s, k).wait_send()
-
-    @pl.loop(0, half - 1)
-    def _(s):
-        for d in range(2):
-            ring_sent(d, s, True)
+            left(gathered.at[0, c], pair_send_sem.at[d, t], pair_sem.at[d, t], pair)
+            left(gathered.at[0, c], ring_send_sem.at[d, t], ring_sem.at[d, t, 0], side[d])
+        for k in range(1, nx):
+            part_copy(t, k).wait_send()
+
+    for t in (half - 1, half):
+        left(gathered.at[0, c], pair_send_sem.at[0, t], pair_sem.at[0, t], pair)
+        for k in range(1, nx):
+            part_copy(t, k).wait_send()
 
     @pl.loop(1, half)
     def _(s):
         for d in range(2):
-            ref = sums.at[d, s]
-            remote(ref, ref, sums_send_sem.at[d, s], sums_sem.at[d, s, 0], side[d]).wait_send()
+            left(sums.at[d, s], sums_send_sem.at[d, s], sums_sem.at[d, s, 0], side[d])
 
     for d in range(2):
-        ring_sent(d, half - 1, False)
-        ref = sums.at[d, 0, :, pl.ds(0, own_cols // 2)]
-        remote(ref, ref, sums_send_sem.at[d, 0], sums_sem.at[d, 0, 0], side[d]).wait_send()
+        left(
+            gathered.at[0, c, :, pl.ds(0, width // 2)], ring_send_sem.at[d, half - 1], ring_sem.at[d, half - 1, 0], side[d]
+        )
+        first = out_cols * sum(starts(d, j) for j in range(OUT_CHUNKS))
+        left(sums.at[d, 0, :, pl.ds(0, first)], sums_send_sem.at[d, 0], sums_sem.at[d, 0, 0], side[d])
     ref = q_in.at[pl.ds(0, nz * CORES - 1)]
-    remote(ref, ref, q_send_sem, q_sem.at[0], pair).wait_send()
-    remote(ref, ref, att_send_sem, att_sem.at[0, 0], pair).wait_send()
-    for b in range(4):
+    left(ref, q_send_sem, q_sem.at[0], pair)
+    left(ref, att_send_sem, att_sem.at[0, 0], pair)
+    for b in range(batches):
         swap_copy(b).wait_send()
         for k in range(1, nx):
             rows_copy(b, k).wait_send()
@@ -432,15 +449,15 @@
             in_specs=[pl.BlockSpec(memory_space=pltpu.SMEM)] + [hbm] * 5,
             out_specs=pl.BlockSpec(memory_space=pltpu.VMEM),
             scratch_shapes=[
-                pltpu.VMEM((half, 2 * CORES, block, width), BF16),
+                pltpu.VMEM((half + 1, 2 * CORES, block, width), BF16),
                 pltpu.VMEM(w_query.shape, BF16),
                 pltpu.VMEM((CORES, feats, own_cols), BF16),
                 pltpu.VMEM(cache_keys.shape, BF16),
                 pltpu.VMEM(cache_values.shape, BF16),
                 pltpu.VMEM((2 * CORES * block, feats), F32),
-                pltpu.VMEM((half, nx, 2 * CORES * seqs, feats), F32),
-                pltpu.VMEM((half, nx - 1, 2 * CORES * seqs, feats), F32),
-                pltpu.VMEM((half, 2 * CORES, seqs, feats), BF16),
+                pltpu.VMEM((half + 1, nx, 2 * CORES * seqs, feats), F32),
+                pltpu.VMEM((half + 1, nx - 1, 2 * CORES * seqs, feats), F32),
+                pltpu.VMEM((half + 1, 2 * CORES, seqs, feats), BF16),
                 pltpu.VMEM((nz * CORES, seqs, feats), BF16),
                 pltpu.VMEM((nz, CORES, seqs, feats), F32),
                 pltpu.VMEM((nz, CORES, seqs, feats), F32),
@@ -453,18 +470,18 @@
                 dma((5,)),
                 dma((2, half)),
                 dma((2, half, IN_CHUNKS)),
-                dma((2, half)),
-                dma((2, half)),
-                dma((half, nx - 1)),
-                dma((half, nx - 1)),
+                dma((2, half + 1)),
+                dma((2, half + 1)),
+                dma((half + 1, nx - 1)),
+                dma((half + 1, nx - 1)),
                 dma(()),
                 dma((nz * CORES,)),
                 dma(()),
                 dma((nz, CORES)),
-                dma((4, nx - 1)),
-                dma((4, nx - 1)),
-                dma((4,)),
-                dma((4,)),
+                dma((nz // PER_BATCH, nx - 1)),
+                dma((nz // PER_BATCH, nx - 1)),
+                dma((nz // PER_BATCH,)),
+                dma((nz // PER_BATCH,)),
                 dma(()),
                 dma(()),
                 dma((2, half)),

time: 125 us -> 122 us (0.976)
  Pallas kernels: 123 us -> 121 us
    pallas_call x1, Pallas kernels: 123 us -> 121 us  [body(): pl.pallas_call(functools.partial(kernel, nz, nx), out_shape=jax.ShapeDtyp...]
where the time goes in v2:
time: 122 us
  Pallas kernels  121 us (99%)
  local copies, waits for them, and re-layouts  1.58 us (1%)
    pallas_call x1, Pallas kernels, body(): pl.pallas_call(functools.partial(kernel, nz, nx), out_shape=jax.ShapeDtyp...  121 us

profile of v2, /device:TPU:33, one launch (start us, length us, event | category | flops | bytes accessed | tf_op | source)
XLA Modules:
  0.0 122.3 jit_solution(10962214135118294391)
XLA Ops:
  0.0 120.7 %decode_step.1 = bf16[16,4608]{1,0:T(8,128)(2,1)} custom-call(s32[4]{0:T(128)} %lengths.1, bf16[16,4608]{1,0:T(8,128)(2,1)} %hidden.1, bf16[4608,384]{1,0:T(8,128)(2,1)} %w_query.1, bf16[384,4608]{1,0:T(8,128)(2,1)} %w_out.1, bf16[4,1024,256]{2,1,0:T(8,128)(2,1)} %keys.1, bf16[4,1024,256]{2,1,0:T(8,128)(2,1)} %values.1), custom_call_target="tpu_custom_call" | custom-call | tf_op jit(solution)/shard_map/decode_step/pallas_call | solution.py:446
  120.7 1.6 %copy.8 = bf16[16,4608]{1,0:T(8,128)(2,1)} copy(bf16[16,4608]{1,0:T(8,128)(2,1)} %decode_step.1) | data formatting | bytes 294912

commit v3 on v2

--- a/solution.py
+++ b/solution.py
@@ -17,7 +17,7 @@
 
 
 def source_offset(v, half):
-    return 0 if v == 0 else half + v // 2 if v % 2 else half - v // 2
+    return half - (v + 1) // 2 if v % 2 else half + v // 2
 
 
 def kernel(
@@ -247,17 +247,24 @@
 
     q_wide[...] = q_in[...].reshape(nz, CORES, seqs, feats).astype(F32)
     heads = CORES * feats // hd
-    for i in range(seqs):
+
+    def scores_of(i):
         rows = jnp.concatenate([q_wide[:, core, i, :] for core in range(CORES)], axis=1)
         query = jnp.concatenate([rows[:, h * hd : (h + 1) * hd] for h in range(heads)], axis=0).astype(BF16)
-        scores = lax.dot_general(query, k_buf[i], (((1,), (1,)), ((), ())), preferred_element_type=F32)
+        return lax.dot_general(query, k_buf[i], (((1,), (1,)), ((), ())), preferred_element_type=F32)
+
+    def probs_of(i, scores):
         scores = scores * F32(hd**-0.5)
         live = lax.broadcasted_iota(jnp.int32, scores.shape, 1) < lengths[i]
         scores = jnp.where(live, scores, F32(-1e30))
         expo = jnp.where(live, jnp.exp(scores - jnp.max(scores, axis=1, keepdims=True)), F32(0.0))
-        probs = (expo / jnp.sum(expo, axis=1, keepdims=True)).astype(BF16)
-        mixed = jnp.dot(probs, v_buf[i], preferred_element_type=F32)
-        wide = jnp.concatenate([mixed[h * nz : (h + 1) * nz, :] for h in range(heads)], axis=1)
+        return (expo / jnp.sum(expo, axis=1, keepdims=True)).astype(BF16)
+
+    scores = [scores_of(i) for i in range(seqs)]
+    probs = [probs_of(i, scores[i]) for i in range(seqs)]
+    mixed = [jnp.dot(probs[i], v_buf[i], preferred_element_type=F32) for i in range(seqs)]
+    for i in range(seqs):
+        wide = jnp.concatenate([mixed[i][h * nz : (h + 1) * nz, :] for h in range(heads)], axis=1)
         for core in range(CORES):
             att_wide[:, core, i, :] = wide[:, core * feats : (core + 1) * feats]
     att_send[...] = att_wide[...].astype(BF16)
@@ -269,42 +276,47 @@
             att_send.at[lax.rem(chip + nz, nz), core], att_in.at[x, v, c], att_send_sem, att_sem.at[v, c], at_z(chip, core)
         )
 
-    for v in [*range(1, nz), 0]:
+    for v in range(nz):
         for r in range(CORES):
-            if v == 0 and r == 0:
+            if v == nz - 1 and r == 0:
                 att_in[x, v, c] = att_send[z, c]
             else:
                 att_copy(v, r).start()
 
-    batches = nz // PER_BATCH
+    own_batch = nz // PER_BATCH + 1
 
     def batch(b):
-        return pl.ds(b * PER_BATCH, PER_BATCH)
+        known = isinstance(b, int)
+        if known and b in (0, own_batch):
+            return (0 if b == 0 else nz - 1), 1
+        return (1, 2) if known and b == 1 else (PER_BATCH * b - 5, PER_BATCH)
 
     def rows_copy(b, k):
-        ref = att_in.at[x, batch(b)]
+        ref = att_in.at[x, pl.ds(*batch(b))]
         return remote(ref, ref, rows_send_sem.at[b, k - 1], rows_sem.at[b, k - 1], at_x(k))
 
     def swap_copy(b):
-        ref = att.at[c, batch(b)]
+        ref = att.at[c, pl.ds(*batch(b))]
         return remote(ref, ref, swap_send_sem.at[b], swap_sem.at[b], pair)
 
     def pass_on(b):
         for k in range(1, nx):
             rows_copy(b, k).wait_recv()
-        for n in range(PER_BATCH):
+        start, count = batch(b)
+        for n in range(count):
             for core in range(CORES):
-                v = b * PER_BATCH + n
+                v = start + n
                 att[c, v, core] = jnp.concatenate(
                     [att_in[g, v, core].astype(F32) for g in range(nx)], axis=0
                 ).astype(BF16)
         swap_copy(b).start()
 
-    for b in range(batches):
-        for v in range(b * PER_BATCH, (b + 1) * PER_BATCH):
+    for b in range(own_batch + 1):
+        start, count = batch(b)
+        for v in range(start, start + count):
             for r in range(CORES):
                 core = lax.rem(c + r, CORES)
-                if v > 0 or r > 0:
+                if v < nz - 1 or r > 0:
                     ref = att_in.at[x, v, core]
                     remote(ref, ref, att_send_sem, att_sem.at[v, core], pair).wait_recv()
         for k in range(1, nx):
@@ -343,10 +355,10 @@
             span = slice(j * out_cols, (j + 1) * out_cols)
             if known and s == 0:
                 d = 0 if starts(0, j) else 1
-                sums[d, 0, :, span] = projected(1, 1, j).astype(BF16)
+                sums[d, 0, :, span] = projected(0, 1, j).astype(BF16)
                 sums_copy(d, 0, j).start()
                 continue
-            both = projected(2 * s, 2, j)
+            both = projected(2 * s - 1, 2, j)
             for d in range(2):
                 term = both[d * tall : (d + 1) * tall]
                 if not known or s > 1 or starts(d, j):
@@ -358,20 +370,25 @@
     pass_on(1)
     swap_copy(0).wait_recv()
     out_step(0)
+    pass_on(2)
+    swap_copy(1).wait_recv()
     out_step(1)
 
-    @pl.loop(1, batches - 1)
+    @pl.loop(2, own_batch - 1)
     def _(b):
         pass_on(b + 1)
         swap_copy(b).wait_recv()
-        out_step(2 * b)
-        out_step(2 * b + 1)
-
-    swap_copy(batches - 1).wait_recv()
+        out_step(2 * b - 2)
+        out_step(2 * b - 1)
+
+    pass_on(own_batch)
+    swap_copy(own_batch - 1).wait_recv()
 
     @pl.loop(half - 2, half)
     def _(s):
         out_step(s)
+
+    swap_copy(own_batch).wait_recv()
 
     def last_copy(j):
         own = pl.ds(pl.multiple_of(c * own_cols + j * out_cols, 128), out_cols)
@@ -381,7 +398,7 @@
 
     for j in range(OUT_CHUNKS):
         span = slice(j * out_cols, (j + 1) * out_cols)
-        term = projected(0, 1, j)
+        term = projected(nz - 1, 1, j)
         for d in range(2):
             sums_copy(d, half - 1, j).wait_recv()
             term = term + sums_in[d, half - 1, :, span].astype(F32)
@@ -422,7 +439,7 @@
     ref = q_in.at[pl.ds(0, nz * CORES - 1)]
     left(ref, q_send_sem, q_sem.at[0], pair)
     left(ref, att_send_sem, att_sem.at[0, 0], pair)
-    for b in range(batches):
+    for b in range(own_batch + 1):
         swap_copy(b).wait_send()
         for k in range(1, nx):
             rows_copy(b, k).wait_send()
@@ -478,10 +495,10 @@
                 dma((nz * CORES,)),
                 dma(()),
                 dma((nz, CORES)),
-                dma((nz // PER_BATCH, nx - 1)),
-                dma((nz // PER_BATCH, nx - 1)),
-                dma((nz // PER_BATCH,)),
-                dma((nz // PER_BATCH,)),
+                dma((nz // PER_BATCH + 2, nx - 1)),
+                dma((nz // PER_BATCH + 2, nx - 1)),
+                dma((nz // PER_BATCH + 2,)),
+                dma((nz // PER_BATCH + 2,)),
                 dma(()),
                 dma(()),
                 dma((2, half)),
@@ -490,7 +507,7 @@
                 dma((OUT_CHUNKS,)),
             ],
             compiler_params=pltpu.CompilerParams(
-                collective_id=0, has_side_effects=True, vmem_limit_bytes=60 * 2**20
+                collective_id=0, has_side_effects=True, vmem_limit_bytes=52 * 2**20
             ),
             name="decode_step",
         )(lengths, hidden_in, w_query, w_out, cache_keys, cache_values)

time: 122 us -> 120 us (0.984)
  Pallas kernels: 121 us -> 118 us
    pallas_call x1, Pallas kernels: 121 us -> 118 us  [body(): pl.pallas_call(functools.partial(kernel, nz, nx), out_shape=jax.ShapeDtyp...]
where the time goes in v3:
time: 120 us
  Pallas kernels  118 us (98%)
  local copies, waits for them, and re-layouts  2.23 us (2%)
    pallas_call x1, Pallas kernels, body(): pl.pallas_call(functools.partial(kernel, nz, nx), out_shape=jax.ShapeDtyp...  118 us

profile of v3, /device:TPU:33, one launch (start us, length us, event | category | flops | bytes accessed | tf_op | source)
XLA Modules:
  0.0 120.2 jit_solution(1618448339782448571)
XLA Ops:
  0.0 0.0 copy-start
  0.0 0.9 copy-done
  0.9 0.0 copy-start.1
  0.9 0.7 copy-done.1
  1.6 118.0 %decode_step.1 = bf16[16,4608]{1,0:T(8,128)(2,1)S(1)} custom-call(s32[4]{0:T(128)S(1)} %copy-done.1, bf16[16,4608]{1,0:T(8,128)(2,1)S(1)} %copy-done, bf16[4608,384]{1,0:T(8,128)(2,1)} %w_query.1, bf16[384,4608]{1,0:T(8,128)(2,1)} %w_out.1, bf16[4,1024,256]{2,1,0:T(8,128)(2,1)} %keys.1, bf16[4,1024,256]{2,1,0:T(8,128)(2,1)} %values.1), custom_call_target="tpu_custom_call" | custom-call | tf_op jit(solution)/shard_map/decode_step/pallas_call | solution.py:463
  119.5 0.7 copy.8
Async XLA Ops:
  0.0 0.9 copy-start
  0.9 0.7 copy-start.1

commit v4 on v3

--- a/solution.py
+++ b/solution.py
@@ -177,7 +177,12 @@
             chip = z if t == half else z + half
         else:
             chip = z - 1 - t if d == 0 else z + 1 + t
-        return remote(q_send.at[t, CORES * d + core], q_in.at[gx], q_send_sem, q_sem.at[gx], at_z(chip, core))
+        slot = 2 * (half - 1 - t) - 1 + d
+        if isinstance(t, int) and t >= half - 1:
+            slot = nz - 1 if t == half else 0
+        return remote(
+            q_send.at[t, CORES * d + core], q_in.at[slot, c], q_send_sem.at[r], q_sem.at[slot, c], at_z(chip, core)
+        )
 
     def send_queries(t):
         rows = blocks(t) * seqs
@@ -190,7 +195,7 @@
         for d in range(blocks(t) // CORES):
             for r in range(CORES):
                 if isinstance(t, int) and t == half and r == 0:
-                    q_in[gx] = q_send[half, c]
+                    q_in[nz - 1, c] = q_send[half, c]
                 else:
                     q_copy(t, d, r).start()
 
@@ -233,23 +238,10 @@
         gather_step(s)
     for j in range(IN_CHUNKS):
         dot_piece(half - 1, j)
-    send_parts(half - 1)
-    send_queries(half - 2)
-    send_queries(half - 1)
-
-    for load in loads[3:]:
-        load.wait()
-
-    @pl.loop(1, nz * CORES)
-    def _(k):
-        ref = q_in.at[lax.rem(gx + k, nz * CORES)]
-        remote(ref, ref, q_send_sem, q_sem.at[lax.rem(gx + k, nz * CORES)], pair).wait_recv()
-
-    q_wide[...] = q_in[...].reshape(nz, CORES, seqs, feats).astype(F32)
     heads = CORES * feats // hd
 
-    def scores_of(i):
-        rows = jnp.concatenate([q_wide[:, core, i, :] for core in range(CORES)], axis=1)
+    def scores_of(i, lo, hi):
+        rows = jnp.concatenate([q_wide[lo:hi, core, i, :] for core in range(CORES)], axis=1)
         query = jnp.concatenate([rows[:, h * hd : (h + 1) * hd] for h in range(heads)], axis=0).astype(BF16)
         return lax.dot_general(query, k_buf[i], (((1,), (1,)), ((), ())), preferred_element_type=F32)
 
@@ -260,28 +252,50 @@
         expo = jnp.where(live, jnp.exp(scores - jnp.max(scores, axis=1, keepdims=True)), F32(0.0))
         return (expo / jnp.sum(expo, axis=1, keepdims=True)).astype(BF16)
 
-    scores = [scores_of(i) for i in range(seqs)]
-    probs = [probs_of(i, scores[i]) for i in range(seqs)]
-    mixed = [jnp.dot(probs[i], v_buf[i], preferred_element_type=F32) for i in range(seqs)]
-    for i in range(seqs):
-        wide = jnp.concatenate([mixed[i][h * nz : (h + 1) * nz, :] for h in range(heads)], axis=1)
-        for core in range(CORES):
-            att_wide[:, core, i, :] = wide[:, core * feats : (core + 1) * feats]
-    att_send[...] = att_wide[...].astype(BF16)
-
     def att_copy(v, r):
         core = lax.rem(c + r, CORES)
-        chip = z - source_offset(v, half)
+        slot = v if v in (0, nz - 1) else v + 1 if v % 2 else v - 1
         return remote(
-            att_send.at[lax.rem(chip + nz, nz), core], att_in.at[x, v, c], att_send_sem, att_sem.at[v, c], at_z(chip, core)
-        )
-
-    for v in range(nz):
-        for r in range(CORES):
-            if v == nz - 1 and r == 0:
-                att_in[x, v, c] = att_send[z, c]
-            else:
-                att_copy(v, r).start()
+            att_send.at[v, core],
+            att_in.at[x, slot, c],
+            att_send_sem.at[r],
+            att_sem.at[slot, c],
+            at_z(z + source_offset(v, half), core),
+        )
+
+    def attend(lo, hi):
+        for v in range(lo, hi):
+            for r in range(CORES):
+                core = lax.rem(c + r, CORES)
+                if v < nz - 1 or r > 0:
+                    ref = q_in.at[v, core]
+                    remote(ref, ref, q_send_sem.at[r], q_sem.at[v, core], pair).wait_recv()
+        q_wide[lo:hi] = q_in[lo:hi].astype(F32)
+        scores = [scores_of(i, lo, hi) for i in range(seqs)]
+        probs = [probs_of(i, scores[i]) for i in range(seqs)]
+        mixed = [jnp.dot(probs[i], v_buf[i], preferred_element_type=F32) for i in range(seqs)]
+        for i in range(seqs):
+            wide = jnp.concatenate(
+                [mixed[i][h * (hi - lo) : (h + 1) * (hi - lo), :] for h in range(heads)], axis=1
+            )
+            for core in range(CORES):
+                att_wide[lo:hi, core, i, :] = wide[:, core * feats : (core + 1) * feats]
+        att_send[lo:hi] = att_wide[lo:hi].astype(BF16)
+        for v in range(lo, hi):
+            for r in range(CORES):
+                if v == nz - 1 and r == 0:
+                    att_in[x, v, c] = att_send[v, c]
+                else:
+                    att_copy(v, r).start()
+
+    send_parts(half - 1)
+    send_queries(half - 2)
+    for load in loads[3:]:
+        load.wait()
+    attend(nz // 2, nz)
+    send_queries(half - 1)
+    attend(nz // 4, nz // 2)
+    attend(0, nz // 4)
 
     own_batch = nz // PER_BATCH + 1
 
@@ -318,7 +332,7 @@
                 core = lax.rem(c + r, CORES)
                 if v < nz - 1 or r > 0:
                     ref = att_in.at[x, v, core]
-                    remote(ref, ref, att_send_sem, att_sem.at[v, core], pair).wait_recv()
+                    remote(ref, ref, att_send_sem.at[r], att_sem.at[v, core], pair).wait_recv()
         for k in range(1, nx):
             rows_copy(b, k).start()
     pass_on(0)
@@ -436,9 +450,10 @@
         )
         first = out_cols * sum(starts(d, j) for j in range(OUT_CHUNKS))
         left(sums.at[d, 0, :, pl.ds(0, first)], sums_send_sem.at[d, 0], sums_sem.at[d, 0, 0], side[d])
-    ref = q_in.at[pl.ds(0, nz * CORES - 1)]
-    left(ref, q_send_sem, q_sem.at[0], pair)
-    left(ref, att_send_sem, att_sem.at[0, 0], pair)
+    for r in range(CORES):
+        ref = q_in.at[pl.ds(0, nz - 1 + r), 0]
+        left(ref, q_send_sem.at[r], q_sem.at[0, 0], pair)
+        left(ref, att_send_sem.at[r], att_sem.at[0, 0], pair)
     for b in range(own_batch + 1):
         swap_copy(b).wait_send()
         for k in range(1, nx):
@@ -475,7 +490,7 @@
                 pltpu.VMEM((half + 1, nx, 2 * CORES * seqs, feats), F32),
                 pltpu.VMEM((half + 1, nx - 1, 2 * CORES * seqs, feats), F32),
                 pltpu.VMEM((half + 1, 2 * CORES, seqs, feats), BF16),
-                pltpu.VMEM((nz * CORES, seqs, feats), BF16),
+                pltpu.VMEM((nz, CORES, seqs, feats), BF16),
                 pltpu.VMEM((nz, CORES, seqs, feats), F32),
                 pltpu.VMEM((nz, CORES, seqs, feats), F32),
                 pltpu.VMEM((nz, CORES, seqs, feats), BF16),
@@ -491,9 +506,9 @@
                 dma((2, half + 1)),
                 dma((half + 1, nx - 1)),
                 dma((half + 1, nx - 1)),
-                dma(()),
-                dma((nz * CORES,)),
-                dma(()),
+                dma((CORES,)),
+                dma((nz, CORES)),
+                dma((CORES,)),
                 dma((nz, CORES)),
                 dma((nz // PER_BATCH + 2, nx - 1)),
                 dma((nz // PER_BATCH + 2, nx - 1)),

time: 120 us -> 121 us (level)
  no operation moved by 1% of the time
where the time goes in v4:
time: 121 us
  Pallas kernels  119 us (98%)
  local copies, waits for them, and re-layouts  2.23 us (2%)
    pallas_call x1, Pallas kernels, body(): pl.pallas_call(functools.partial(kernel, nz, nx), out_shape=jax.ShapeDtyp...  119 us

profile of v4, /device:TPU:33, one launch (start us, length us, event | category | flops | bytes accessed | tf_op | source)
XLA Modules:
  0.0 121.0 jit_solution(10626671582324012762)
XLA Ops:
  0.0 0.0 copy-start
  0.0 0.9 copy-done
  0.9 0.0 copy-start.1
  0.9 0.7 copy-done.1
  1.6 118.8 %decode_step.1 = bf16[16,4608]{1,0:T(8,128)(2,1)S(1)} custom-call(s32[4]{0:T(128)S(1)} %copy-done.1, bf16[16,4608]{1,0:T(8,128)(2,1)S(1)} %copy-done, bf16[4608,384]{1,0:T(8,128)(2,1)} %w_query.1, bf16[384,4608]{1,0:T(8,128)(2,1)} %w_out.1, bf16[4,1024,256]{2,1,0:T(8,128)(2,1)} %keys.1, bf16[4,1024,256]{2,1,0:T(8,128)(2,1)} %values.1), custom_call_target="tpu_custom_call" | custom-call | tf_op jit(solution)/shard_map/decode_step/pallas_call | solution.py:478
  120.4 0.7 copy.8
Async XLA Ops:
  0.0 0.9 copy-start
  0.9 0.7 copy-start.1

commit v5 on v4

--- a/solution.py
+++ b/solution.py
@@ -10,7 +10,7 @@
 MESH = pl.DeviceIdType.MESH
 CORES = 2
 IN_CHUNKS = 6
-OUT_CHUNKS = 9
+OUT_CHUNKS = 6
 PER_BATCH = 4
 F32 = jnp.float32
 BF16 = jnp.bfloat16
@@ -292,9 +292,8 @@
     send_queries(half - 2)
     for load in loads[3:]:
         load.wait()
-    attend(nz // 2, nz)
     send_queries(half - 1)
-    attend(nz // 4, nz // 2)
+    attend(nz // 4, nz)
     attend(0, nz // 4)
 
     own_batch = nz // PER_BATCH + 1
@@ -522,7 +521,7 @@
                 dma((OUT_CHUNKS,)),
             ],
             compiler_params=pltpu.CompilerParams(
-                collective_id=0, has_side_effects=True, vmem_limit_bytes=52 * 2**20
+                collective_id=0, has_side_effects=True, vmem_limit_bytes=215 * 2**18
             ),
             name="decode_step",
         )(lengths, hidden_in, w_query, w_out, cache_keys, cache_values)

time: 121 us -> 119 us (0.983)
  Pallas kernels: 119 us -> 117 us
    pallas_call x1, Pallas kernels: 119 us -> 117 us  [body(): pl.pallas_call(functools.partial(kernel, nz, nx), out_shape=jax.ShapeDtyp...]
where the time goes in v5:
time: 119 us; the launch traced here: 118 us
  Pallas kernels  117 us (98%)
  local copies, waits for them, and re-layouts  1.32 us (1%)
    pallas_call x1, Pallas kernels, body(): pl.pallas_call(functools.partial(kernel, nz, nx), out_shape=jax.ShapeDtyp...  117 us

profile of v5, /device:TPU:33, one launch (start us, length us, event | category | flops | bytes accessed | tf_op | source)
XLA Modules:
  0.0 118.5 jit_solution(8646616539548149294)
XLA Ops:
  0.0 0.0 copy-start
  0.0 0.7 copy-done
  0.7 117.2 %decode_step.1 = bf16[16,4608]{1,0:T(8,128)(2,1)S(1)} custom-call(s32[4]{0:T(128)S(1)} %copy-done, bf16[16,4608]{1,0:T(8,128)(2,1)} %hidden.1, bf16[4608,384]{1,0:T(8,128)(2,1)} %w_query.1, bf16[384,4608]{1,0:T(8,128)(2,1)} %w_out.1, bf16[4,1024,256]{2,1,0:T(8,128)(2,1)} %keys.1, bf16[4,1024,256]{2,1,0:T(8,128)(2,1)} %values.1), custom_call_target="tpu_custom_call" | custom-call | tf_op jit(solution)/shard_map/decode_step/pallas_call | solution.py:477
  117.8 0.7 copy.8
Async XLA Ops:
  0.0 0.7 copy-start

commit v6 on v5

--- a/solution.py
+++ b/solution.py
@@ -59,6 +59,8 @@
     q_sem,
     att_send_sem,
     att_sem,
+    far_send_sem,
+    far_sem,
     rows_send_sem,
     rows_sem,
     swap_send_sem,
@@ -263,6 +265,10 @@
             at_z(z + source_offset(v, half), core),
         )
 
+    def far_copy(k, core):
+        device = {**at_z(z + half, core), **at_x(k)}
+        return remote(att_send.at[0, core], att_in.at[x, 0, c], far_send_sem, far_sem.at[k - 1, c], device)
+
     def attend(lo, hi):
         for v in range(lo, hi):
             for r in range(CORES):
@@ -287,6 +293,9 @@
                     att_in[x, v, c] = att_send[v, c]
                 else:
                     att_copy(v, r).start()
+                if v == 0:
+                    for k in range(1, nx):
+                        far_copy(k, lax.rem(c + r, CORES)).start()
 
     send_parts(half - 1)
     send_queries(half - 2)
@@ -314,7 +323,12 @@
 
     def pass_on(b):
         for k in range(1, nx):
-            rows_copy(b, k).wait_recv()
+            if isinstance(b, int) and b == 0:
+                for core in range(CORES):
+                    ref = att_in.at[lax.rem(x - k + nx, nx), 0, core]
+                    remote(ref, ref, far_send_sem, far_sem.at[k - 1, core], pair).wait_recv()
+            else:
+                rows_copy(b, k).wait_recv()
         start, count = batch(b)
         for n in range(count):
             for core in range(CORES):
@@ -324,7 +338,7 @@
                 ).astype(BF16)
         swap_copy(b).start()
 
-    for b in range(own_batch + 1):
+    for b in [1, 0, *range(2, own_batch + 1)]:
         start, count = batch(b)
         for v in range(start, start + count):
             for r in range(CORES):
@@ -332,9 +346,11 @@
                 if v < nz - 1 or r > 0:
                     ref = att_in.at[x, v, core]
                     remote(ref, ref, att_send_sem.at[r], att_sem.at[v, core], pair).wait_recv()
-        for k in range(1, nx):
-            rows_copy(b, k).start()
-    pass_on(0)
+        if b == 0:
+            pass_on(0)
+        else:
+            for k in range(1, nx):
+                rows_copy(b, k).start()
     loads[2].wait()
     wo_copy.wait_recv()
 
@@ -455,8 +471,10 @@
         left(ref, att_send_sem.at[r], att_sem.at[0, 0], pair)
     for b in range(own_batch + 1):
         swap_copy(b).wait_send()
-        for k in range(1, nx):
-            rows_copy(b, k).wait_send()
+        if b > 0:
+            for k in range(1, nx):
+                rows_copy(b, k).wait_send()
+    left(q_in.at[pl.ds(0, nx - 1)], far_send_sem, far_sem.at[0, 0], pair)
     wo_copy.wait_send()
     for j in range(OUT_CHUNKS):
         last_copy(j).wait_send()
@@ -509,6 +527,8 @@
                 dma((nz, CORES)),
                 dma((CORES,)),
                 dma((nz, CORES)),
+                dma(()),
+                dma((nx - 1, CORES)),
                 dma((nz // PER_BATCH + 2, nx - 1)),
                 dma((nz // PER_BATCH + 2, nx - 1)),
                 dma((nz // PER_BATCH + 2,)),

time: 119 us -> 117 us (0.983)
  no operation moved by 1% of the time
where the time goes in v6:
time: 117 us
  Pallas kernels  116 us (99%)
  local copies, waits for them, and re-layouts  1.32 us (1%)
    pallas_call x1, Pallas kernels, body(): pl.pallas_call(functools.partial(kernel, nz, nx), out_shape=jax.ShapeDtyp...  116 us

profile of v6, /device:TPU:33, one launch (start us, length us, event | category | flops | bytes accessed | tf_op | source)
XLA Modules:
  0.0 117.4 jit_solution(6042101477369112962)
XLA Ops:
  0.0 0.0 copy-start
  0.0 0.7 copy-done
  0.7 116.0 %decode_step.1 = bf16[16,4608]{1,0:T(8,128)(2,1)S(1)} custom-call(s32[4]{0:T(128)S(1)} %copy-done, bf16[16,4608]{1,0:T(8,128)(2,1)} %hidden.1, bf16[4608,384]{1,0:T(8,128)(2,1)} %w_query.1, bf16[384,4608]{1,0:T(8,128)(2,1)} %w_out.1, bf16[4,1024,256]{2,1,0:T(8,128)(2,1)} %keys.1, bf16[4,1024,256]{2,1,0:T(8,128)(2,1)} %values.1), custom_call_target="tpu_custom_call" | custom-call | tf_op jit(solution)/shard_map/decode_step/pallas_call | solution.py:495
  116.7 0.7 copy.8
Async XLA Ops:
  0.0 0.7 copy-start

commit v7 on v6

--- a/solution.py
+++ b/solution.py
@@ -338,7 +338,7 @@
                 ).astype(BF16)
         swap_copy(b).start()
 
-    for b in [1, 0, *range(2, own_batch + 1)]:
+    for b in [*range(3, own_batch + 1), 1, 2, 0]:
         start, count = batch(b)
         for v in range(start, start + count):
             for r in range(CORES):

time: 117 us -> 118 us (level)
  no operation moved by 1% of the time
where the time goes in v7:
time: 118 us
  Pallas kernels  116 us (98%)
  local copies, waits for them, and re-layouts  1.32 us (1%)
    pallas_call x1, Pallas kernels, body(): pl.pallas_call(functools.partial(kernel, nz, nx), out_shape=jax.ShapeDtyp...  116 us

profile of v7, /device:TPU:33, one launch (start us, length us, event | category | flops | bytes accessed | tf_op | source)
XLA Modules:
  0.0 117.6 jit_solution(9367906770696477813)
XLA Ops:
  0.0 0.0 copy-start
  0.0 0.7 copy-done
  0.7 116.3 %decode_step.1 = bf16[16,4608]{1,0:T(8,128)(2,1)S(1)} custom-call(s32[4]{0:T(128)S(1)} %copy-done, bf16[16,4608]{1,0:T(8,128)(2,1)} %hidden.1, bf16[4608,384]{1,0:T(8,128)(2,1)} %w_query.1, bf16[384,4608]{1,0:T(8,128)(2,1)} %w_out.1, bf16[4,1024,256]{2,1,0:T(8,128)(2,1)} %keys.1, bf16[4,1024,256]{2,1,0:T(8,128)(2,1)} %values.1), custom_call_target="tpu_custom_call" | custom-call | tf_op jit(solution)/shard_map/decode_step/pallas_call | solution.py:495
  117.0 0.7 copy.8
Async XLA Ops:
  0.0 0.7 copy-start
